TPU v7x, 256 devices: a whole 4x4x8 slice. The times are simulated.
256 devices in a mesh: bank: 16 (over y, x), zero: 16 (over z, core).
Axes of the slice: x: 4, y: 4, z: 8, core: 2. Of those that a mesh axis runs over, the one named last changes fastest.
Arguments:
- w_down: float32 [64, 1024, 2048], P('bank', None, 'zero'), may hold values from -0.25 to 0.25
- avg_down: bfloat16 [64, 1024, 2048], P('bank', None, 'zero'), may hold values from -0.09375 to 0.09375
- router_weight: float32 [2048, 64], P('zero', 'bank'), may hold values from -0.125 to 0.125
- router_gain: float32 [2048], P('zero'), may hold values from 0.25 to 1.75
Outputs:
- serve_down: bfloat16 [64, 1024, 2048], P('bank')
- scale_down: float32 [64, 1024], P('bank')
- serve_router: bfloat16 [2048, 64], replicated
All inputs are finite; a program needn't handle non-finite values.
Results may differ from a plain program's by a relative error of at most 0.001.
Values may be sent and summed in bfloat16 or wider, within the bound.
No kernel may reach another device: no remote copies, remote signals or barrier semaphores. Data moves between devices by JAX's collectives and lax.ppermute only.
A program may use at most 128 MiB of HBM per device.

v0:
```python
import jax
import jax.numpy as jnp
from jax import lax
from jax.sharding import PartitionSpec as P


def copy_for_each(x, axis):
    copies = jnp.broadcast_to(x, (lax.axis_size(axis), *x.shape))
    return lax.all_to_all(copies, axis, split_axis=0, concat_axis=0, tiled=True)


def over_copies(x, axis):
    return copy_for_each(x, axis).sum(axis=0)


def in_order(parts, dim):
    dims = list(parts.shape[1:])
    dims[dim] *= parts.shape[0]
    return jnp.moveaxis(parts, 0, dim).reshape(dims)


def gather_directly(x, axis, dim):
    parts = copy_for_each(x, axis)
    return in_order(parts, dim)


def shards(w_down, avg_down, router_weight, router_gain):
    fresh_down = w_down + avg_down.astype(jnp.float32)
    total_down = over_copies(jnp.sum(fresh_down * fresh_down, axis=2), "zero")
    scale_down = jnp.sqrt(total_down)
    narrow_down = (fresh_down / jnp.expand_dims(scale_down, 2)).astype(jnp.bfloat16)
    serve_down = lax.all_gather(narrow_down, "zero", axis=2, tiled=True)
    part_router = (router_weight * router_gain[:, None]).astype(jnp.bfloat16)
    row_router = gather_directly(part_router, "zero", 0)
    serve_router = gather_directly(row_router, "bank", 1)
    return (serve_down, scale_down, serve_router)


def solution(mesh):
    return jax.shard_map(
        shards,
        mesh=mesh,
        in_specs=(P("bank", None, "zero"), P("bank", None, "zero"), P("zero", "bank"), P("zero")),
        out_specs=(P("bank", None, None), P("bank", None), P()),
        check_vma=False,
    )
```

profile of v0, /device:TPU:1, one launch (start us, length us, event | category | flops | bytes accessed | tf_op | source)
XLA Modules:
  0.0 152.9 jit_solution(14177765800500866044)
XLA Ops:
  7.2 0.0 copy-start
  7.2 0.0 copy-start.1
  7.2 0.0 all-gather.2.cloned.1.call-start
  7.2 2.6 %multiply_reduce_fusion = f32[4,1024]{1,0:T(4,128)S(1)} fusion(f32[4,1024,128]{2,1,0:T(8,128)} %param.4, bf16[4,1024,128]{2,1,0:T(8,128)(2,1)} %param.5), kind=kLoop, calls=%fused_computation.1 | loop fusion | flops 2093056 | bytes 3162112 | tf_op jit(solution)/shard_map/reduce_sum | solution.py:29
  9.9 21.4 %all_to_all.15 = f32[16,4,1024]{2,1,0:T(4,128)S(1)} all-to-all(f32[16,4,1024]{2,1,0:T(4,128)S(1)} %broadcast_in_dim.11), channel_id=1, replica_groups=mesh['bank'=16,'zero'=16] {'zero'}, dimensions={0} | all-to-all | bytes 524288 | tf_op jit(solution)/shard_map/all_to_all | solution.py:9
  31.3 0.1 reduce_sum.19
  31.3 0.0 copy-done
  31.4 0.0 copy-done.1
  31.4 0.0 copy-start.2
  31.4 0.0 copy-start.3
  31.4 0.0 copy-start.4
  31.4 1.5 divide_convert_fusion
  32.9 0.0 copy-done.2
  32.9 0.0 all-gather.2.cloned.1.call-update
  32.9 0.0 copy-done.3
  33.0 0.0 copy-done.4
  33.0 10.1 %all_to_all.16 = bf16[16,128,4]{1,2,0:T(4,128)(2,1)S(1)} all-to-all(bf16[16,128,4]{1,2,0:T(4,128)(2,1)S(1)} %broadcast_in_dim.12), channel_id=1, replica_groups=mesh['bank'=16,'zero'=16] {'zero'}, dimensions={0} | all-to-all | bytes 32768 | tf_op jit(solution)/shard_map/all_to_all | solution.py:9
  43.1 0.1 broadcast_in_dim.13
  43.2 14.7 %all_to_all.17 = bf16[16,2048,4]{1,2,0:T(4,128)(2,1)S(1)} all-to-all(bf16[16,2048,4]{1,2,0:T(4,128)(2,1)S(1)} %broadcast_in_dim.13), channel_id=1, replica_groups=mesh['bank'=16,'zero'=16] {'bank'}, dimensions={0} | all-to-all | bytes 524288 | tf_op jit(solution)/shard_map/all_to_all | solution.py:9
  57.9 0.8 reshape.17
  58.6 73.3 %all-gather.2.cloned.1.call-done = bf16[4,1024,2048]{2,1,0:T(8,128)(2,1)} async-done(((bf16[4,1024,128]{2,1,0:T(8,128)(2,1)}), bf16[4,1024,2048]{2,1,0:T(8,128)(2,1)}) %all-gather.2.cloned.1.call-update) | async-done | bytes 16777232 | tf_op jit(solution)/shard_map/all_gather | solution.py:32
  131.9 14.2 %copy.10 = bf16[4,1024,2048]{2,1,0:T(8,128)(2,1)} copy(bf16[4,1024,2048]{2,1,0:T(8,128)(2,1)} %all-gather.2.cloned.1.call-done) | data formatting | bytes 33554432
  (4 shorter events, 0.1 us)
Async XLA Ops:
  7.2 24.2 %copy-start = (f32[4,1024,128]{2,1,0:T(8,128)S(1)}, f32[4,1024,128]{2,1,0:T(8,128)}, u32[]{:S(2)}) copy-start(f32[4,1024,128]{2,1,0:T(8,128)} %param.4) | copy-start | bytes 6291460
  7.2 24.2 %copy-start.1 = (bf16[4,1024,128]{2,1,0:T(8,128)(2,1)S(1)}, bf16[4,1024,128]{2,1,0:T(8,128)(2,1)}, u32[]{:S(2)}) copy-start(bf16[4,1024,128]{2,1,0:T(8,128)(2,1)} %param.5) | copy-start | bytes 3145732
  7.2 124.7 %all-gather.2.cloned.1.call-start = ((), (), s32[]{:S(2)}) async-start(), calls=%async_computation.3 | async-start | bytes 17825792 | tf_op jit(solution)/shard_map/all_gather | solution.py:32
  31.4 1.6 %copy-start.2 = (f32[4,1024]{1,0:T(4,128)}, f32[4,1024]{1,0:T(4,128)S(1)}, u32[]{:S(2)}) copy-start(f32[4,1024]{1,0:T(4,128)S(1)} %sqrt.7) | copy-start | bytes 49156
  31.4 1.6 %copy-start.3 = (f32[128,4]{0,1:T(4,128)S(1)}, f32[128,4]{0,1:T(4,128)}, u32[]{:S(2)}) copy-start(f32[128,4]{0,1:T(4,128)} %param.6) | copy-start | bytes 6148
  31.4 1.6 %copy-start.4 = (f32[128]{0:T(128)S(1)}, f32[128]{0:T(128)}, u32[]{:S(2)}) copy-start(f32[128]{0:T(128)} %param.7) | copy-start | bytes 1540
Sparse Core Ops, SparseCore 0:
  33.1 98.8 all-gather.1
where the time goes:
time: 153 us
  waiting for transfers between devices  73.3 us (48%)
  blocking collectives  46.1 us (30%)
  local copies, waits for them, and re-layouts  15.1 us (10%)
  between operations  14.1 us (9%)
  other arithmetic  4.21 us (3%)
    all_gather x1, waiting for transfers between devices, shards(): serve_down = lax.all_gather(narrow_down, 'zero', axis=2, tiled=True)  73.3 us
    all_to_all x3, blocking collectives, copy_for_each(): return lax.all_to_all(copies, axis, split_axis=0, concat_axis=0, tiled=True)  46.1 us
    unnamed x11, local copies, waits for them, and re-layouts  14.2 us
  transfers between devices with their start and end apart: 1, of which 1 were waited for; matrix products, arithmetic and copies ran while one was open for 1% of the time, Pallas kernels for 0%

commit v1 on v0

--- a/solution.py
+++ b/solution.py
@@ -2,6 +2,28 @@
 import jax.numpy as jnp
 from jax import lax
 from jax.sharding import PartitionSpec as P
+
+
+def joined_along(parts, dim):
+    lengths = list(parts.shape[1:])
+    lengths[dim] *= parts.shape[0]
+    return jnp.moveaxis(parts, 0, dim).reshape(lengths)
+
+
+def gather_around(x, axis, dim):
+    devices = lax.axis_size(axis)
+    pairs = [(i, (i + 1) % devices) for i in range(devices)]
+    back = [(b, a) for a, b in pairs]
+    lower, upper = ([], [])
+    for hop in range(devices - 1):
+        if hop % 2 == 0:
+            lower.append(lax.ppermute(lower[-1] if lower else x, axis, pairs))
+        else:
+            upper.append(lax.ppermute(upper[-1] if upper else x, axis, back))
+    blocks = jnp.stack([*lower[::-1], x, *upper])
+    shift = lax.axis_index(axis) - len(lower)
+    blocks = blocks[(jnp.arange(devices) - shift) % devices]
+    return joined_along(blocks, dim)
 
 
 def copy_for_each(x, axis):
@@ -29,7 +51,7 @@
     total_down = over_copies(jnp.sum(fresh_down * fresh_down, axis=2), "zero")
     scale_down = jnp.sqrt(total_down)
     narrow_down = (fresh_down / jnp.expand_dims(scale_down, 2)).astype(jnp.bfloat16)
-    serve_down = lax.all_gather(narrow_down, "zero", axis=2, tiled=True)
+    serve_down = gather_around(narrow_down, "zero", 2)
     part_router = (router_weight * router_gain[:, None]).astype(jnp.bfloat16)
     row_router = gather_directly(part_router, "zero", 0)
     serve_router = gather_directly(row_router, "bank", 1)

time: 153 us -> 224 us (1.46)
  starting transfers between devices: 0.04 us -> 44.7 us
  local copies, waits for them, and re-layouts: 15.1 us -> 57.7 us
  between operations: 14.1 us -> 0.73 us
  waiting for transfers between devices: 73.3 us -> 70.4 us
    all_gather x1 -> x0, waiting for transfers between devices: 73.3 us -> none  [shards(): serve_down = lax.all_gather(narrow_down, 'zero', axis=2, tiled=True)]
    ppermute x0 -> x15, waiting for transfers between devices: none -> 62.3 us  [the longest x8 56.9 us: gather_around(): lower.append(lax.ppermute(lower[-1] if lower else x, axis, pairs))]
    ppermute x0 -> x15, starting transfers between devices: none -> 37.9 us  [the longest x7 20.5 us: gather_around(): upper.append(lax.ppermute(upper[-1] if upper else x, axis, back))]
    reshape x0 -> x1, local copies, waits for them, and re-layouts: none -> 14.4 us  [joined_along(): return jnp.moveaxis(parts, 0, dim).reshape(lengths)]
    unnamed x11 -> x39, local copies, waits for them, and re-layouts: 14.2 us -> 27.6 us
    gather x0 -> x1, local copies, waits for them, and re-layouts: none -> 13 us  [gather_around(): blocks = blocks[(jnp.arange(devices) - shift) % devices]]
    all_to_all x0 -> x1, waiting for transfers between devices: none -> 8.07 us  [copy_for_each(): return lax.all_to_all(copies, axis, split_axis=0, concat_axis=0, tiled=True)]
    all_to_all x0 -> x1, starting transfers between devices: none -> 6.75 us  [copy_for_each(): return lax.all_to_all(copies, axis, split_axis=0, concat_axis=0, tiled=True)]
  transfers between devices with their start and end apart: 1 -> 16, of which waited for: 1 -> 13; matrix products, arithmetic and copies ran while one was open for 1% -> 13% of each run, Pallas kernels for 0% -> 0%
where the time goes in v1:
time: 224 us; the launch traced here: 223 us
  waiting for transfers between devices  70.4 us (31%)
  local copies, waits for them, and re-layouts  57.7 us (26%)
  starting transfers between devices  44.7 us (20%)
  blocking collectives  44.4 us (20%)
  other arithmetic  5.46 us (2%)
    ppermute x8, waiting for transfers between devices, gather_around(): lower.append(lax.ppermute(lower[-1] if lower else x, axis, pairs))  56.9 us
    all_to_all x2, blocking collectives, copy_for_each(): return lax.all_to_all(copies, axis, split_axis=0, concat_axis=0, tiled=True)  44.4 us
    unnamed x39, local copies, waits for them, and re-layouts  27.6 us
    ppermute x7, starting transfers between devices, gather_around(): upper.append(lax.ppermute(upper[-1] if upper else x, axis, back))  20.5 us
    ppermute x8, starting transfers between devices, gather_around(): lower.append(lax.ppermute(lower[-1] if lower else x, axis, pairs))  17.5 us
    reshape x1, local copies, waits for them, and re-layouts, joined_along(): return jnp.moveaxis(parts, 0, dim).reshape(lengths)  14.4 us
    gather x1, local copies, waits for them, and re-layouts, gather_around(): blocks = blocks[(jnp.arange(devices) - shift) % devices]  13 us
    all_to_all x1, waiting for transfers between devices, copy_for_each(): return lax.all_to_all(copies, axis, split_axis=0, concat_axis=0, tiled=True)  8.07 us
  transfers between devices with their start and end apart: 16, of which 13 were waited for; matrix products, arithmetic and copies ran while one was open for 13% of the time, Pallas kernels for 0%

profile of v1, /device:TPU:1, one launch (start us, length us, event | category | flops | bytes accessed | tf_op | source)
XLA Modules:
  0.0 223.4 jit_solution(8070513788813625847)
XLA Ops:
  0.6 2.5 %multiply_reduce_fusion = f32[4,1024]{1,0:T(4,128)S(1)} fusion(f32[4,1024,128]{2,1,0:T(8,128)} %param.4, bf16[4,1024,128]{2,1,0:T(8,128)(2,1)} %param.5), kind=kLoop, calls=%fused_computation.3 | loop fusion | flops 2093056 | bytes 3162112 | tf_op jit(solution)/shard_map/reduce_sum | solution.py:51
  3.2 21.4 %all_to_all.15 = f32[16,4,1024]{2,1,0:T(4,128)S(1)} all-to-all(f32[16,4,1024]{2,1,0:T(4,128)S(1)} %broadcast_in_dim.12), channel_id=1, replica_groups=mesh['bank'=16,'zero'=16] {'zero'}, dimensions={0} | all-to-all | bytes 524288 | tf_op jit(solution)/shard_map/all_to_all | solution.py:31
  24.6 2.2 divide_convert_fusion
  26.9 11.7 %collective-permute-done = bf16[4,1024,128]{2,1,0:T(8,128)(2,1)S(1)} collective-permute-done((bf16[4,1024,128]{2,1,0:T(8,128)(2,1)S(1)}, bf16[4,1024,128]{2,1,0:T(8,128)(2,1)S(1)}, u32[]{:S(2)}, u32[]{:S(2)}) %collective-permute-start) | collective-permute-done | bytes 1048608 | tf_op jit(solution)/shard_map/ppermute | solution.py:20
  38.6 2.5 %collective-permute-start.1 = (bf16[4,1024,128]{2,1,0:T(8,128)(2,1)S(1)}, bf16[4,1024,128]{2,1,0:T(8,128)(2,1)S(1)}, u32[]{:S(2)}, u32[]{:S(2)}) collective-permute-start(bf16[4,1024,128]{2,1,0:T(8,128)(2,1)S(1)} %collective-permute-done), channel_id=1, source_target_pairs={{0,1},{1,2},{2,3},{3,4},{4,5},{5,6},{6,7},{7,8},{8,9},{9,10},{10,1... | collective-permute-start | bytes 3145736 | tf_op jit(solution)/shard_map/ppermute | solution.py:20
  41.9 10.9 %collective-permute-done.1 = bf16[4,1024,128]{2,1,0:T(8,128)(2,1)S(1)} collective-permute-done((bf16[4,1024,128]{2,1,0:T(8,128)(2,1)S(1)}, bf16[4,1024,128]{2,1,0:T(8,128)(2,1)S(1)}, u32[]{:S(2)}, u32[]{:S(2)}) %collective-permute-start.1) | collective-permute-done | bytes 1048608 | tf_op jit(solution)/shard_map/ppermute | solution.py:20
  52.8 2.5 %collective-permute-start.2 = (bf16[4,1024,128]{2,1,0:T(8,128)(2,1)S(1)}, bf16[4,1024,128]{2,1,0:T(8,128)(2,1)S(1)}, u32[]{:S(2)}, u32[]{:S(2)}) collective-permute-start(bf16[4,1024,128]{2,1,0:T(8,128)(2,1)S(1)} %collective-permute-done.1), channel_id=1, source_target_pairs={{0,1},{1,2},{2,3},{3,4},{4,5},{5,6},{6,7},{7,8},{8,9},{9,10},{10,1... | collective-permute-start | bytes 3145736 | tf_op jit(solution)/shard_map/ppermute | solution.py:20
  55.6 1.8 collective-permute-start.9
  57.4 9.6 %collective-permute-done.2 = bf16[4,1024,128]{2,1,0:T(8,128)(2,1)S(1)} collective-permute-done((bf16[4,1024,128]{2,1,0:T(8,128)(2,1)S(1)}, bf16[4,1024,128]{2,1,0:T(8,128)(2,1)S(1)}, u32[]{:S(2)}, u32[]{:S(2)}) %collective-permute-start.2) | collective-permute-done | bytes 1048608 | tf_op jit(solution)/shard_map/ppermute | solution.py:20
  67.0 2.5 %collective-permute-start.3 = (bf16[4,1024,128]{2,1,0:T(8,128)(2,1)S(1)}, bf16[4,1024,128]{2,1,0:T(8,128)(2,1)S(1)}, u32[]{:S(2)}, u32[]{:S(2)}) collective-permute-start(bf16[4,1024,128]{2,1,0:T(8,128)(2,1)S(1)} %collective-permute-done.2), channel_id=1, source_target_pairs={{0,1},{1,2},{2,3},{3,4},{4,5},{5,6},{6,7},{7,8},{8,9},{9,10},{10,1... | collective-permute-start | bytes 3145736 | tf_op jit(solution)/shard_map/ppermute | solution.py:20
  70.1 2.7 %collective-permute-start.10 = (bf16[4,1024,128]{2,1,0:T(8,128)(2,1)S(1)}, bf16[4,1024,128]{2,1,0:T(8,128)(2,1)S(1)}, u32[]{:S(2)}, u32[]{:S(2)}) collective-permute-start(bf16[4,1024,128]{2,1,0:T(8,128)(2,1)S(1)} %collective-permute-done.9), channel_id=1, source_target_pairs={{1,0},{2,1},{3,2},{4,3},{5,4},{6,5},{7,6},{8,7},{9,8},{10,9},{11,1... | collective-permute-start | bytes 3145736 | tf_op jit(solution)/shard_map/ppermute | solution.py:22
  72.9 8.4 %collective-permute-done.3 = bf16[4,1024,128]{2,1,0:T(8,128)(2,1)S(1)} collective-permute-done((bf16[4,1024,128]{2,1,0:T(8,128)(2,1)S(1)}, bf16[4,1024,128]{2,1,0:T(8,128)(2,1)S(1)}, u32[]{:S(2)}, u32[]{:S(2)}) %collective-permute-start.3) | collective-permute-done | bytes 1048608 | tf_op jit(solution)/shard_map/ppermute | solution.py:20
  81.3 2.5 %collective-permute-start.4 = (bf16[4,1024,128]{2,1,0:T(8,128)(2,1)S(1)}, bf16[4,1024,128]{2,1,0:T(8,128)(2,1)S(1)}, u32[]{:S(2)}, u32[]{:S(2)}) collective-permute-start(bf16[4,1024,128]{2,1,0:T(8,128)(2,1)S(1)} %collective-permute-done.3), channel_id=1, source_target_pairs={{0,1},{1,2},{2,3},{3,4},{4,5},{5,6},{6,7},{7,8},{8,9},{9,10},{10,1... | collective-permute-start | bytes 3145736 | tf_op jit(solution)/shard_map/ppermute | solution.py:20
  83.8 0.9 collective-permute-done.10
  84.6 3.6 %collective-permute-start.11 = (bf16[4,1024,128]{2,1,0:T(8,128)(2,1)S(1)}, bf16[4,1024,128]{2,1,0:T(8,128)(2,1)S(1)}, u32[]{:S(2)}, u32[]{:S(2)}) collective-permute-start(bf16[4,1024,128]{2,1,0:T(8,128)(2,1)S(1)} %collective-permute-done.10), channel_id=1, source_target_pairs={{1,0},{2,1},{3,2},{4,3},{5,4},{6,5},{7,6},{8,7},{9,8},{10,9},{11,1... | collective-permute-start | bytes 3145736 | tf_op jit(solution)/shard_map/ppermute | solution.py:22
  88.3 7.2 %collective-permute-done.4 = bf16[4,1024,128]{2,1,0:T(8,128)(2,1)S(1)} collective-permute-done((bf16[4,1024,128]{2,1,0:T(8,128)(2,1)S(1)}, bf16[4,1024,128]{2,1,0:T(8,128)(2,1)S(1)}, u32[]{:S(2)}, u32[]{:S(2)}) %collective-permute-start.4) | collective-permute-done | bytes 1048608 | tf_op jit(solution)/shard_map/ppermute | solution.py:20
  95.5 2.5 %collective-permute-start.5 = (bf16[4,1024,128]{2,1,0:T(8,128)(2,1)S(1)}, bf16[4,1024,128]{2,1,0:T(8,128)(2,1)S(1)}, u32[]{:S(2)}, u32[]{:S(2)}) collective-permute-start(bf16[4,1024,128]{2,1,0:T(8,128)(2,1)S(1)} %collective-permute-done.4), channel_id=1, source_target_pairs={{0,1},{1,2},{2,3},{3,4},{4,5},{5,6},{6,7},{7,8},{8,9},{9,10},{10,1... | collective-permute-start | bytes 3145736 | tf_op jit(solution)/shard_map/ppermute | solution.py:20
  98.0 1.2 collective-permute-done.11
  99.2 1.0 copy-done.6
  100.1 4.6 %collective-permute-start.12 = (bf16[4,1024,128]{2,1,0:T(8,128)(2,1)S(1)}, bf16[4,1024,128]{2,1,0:T(8,128)(2,1)}, u32[]{:S(2)}, u32[]{:S(2)}) collective-permute-start(bf16[4,1024,128]{2,1,0:T(8,128)(2,1)S(1)} %collective-permute-done.11), channel_id=1, source_target_pairs={{1,0},{2,1},{3,2},{4,3},{5,4},{6,5},{7,6},{8,7},{9,8},{10,9},{11,1... | collective-permute-start | bytes 3145736 | tf_op jit(solution)/shard_map/ppermute | solution.py:22
  104.7 5.0 %collective-permute-done.5 = bf16[4,1024,128]{2,1,0:T(8,128)(2,1)S(1)} collective-permute-done((bf16[4,1024,128]{2,1,0:T(8,128)(2,1)S(1)}, bf16[4,1024,128]{2,1,0:T(8,128)(2,1)S(1)}, u32[]{:S(2)}, u32[]{:S(2)}) %collective-permute-start.5) | collective-permute-done | bytes 1048608 | tf_op jit(solution)/shard_map/ppermute | solution.py:20
  109.7 2.5 %collective-permute-start.6 = (bf16[4,1024,128]{2,1,0:T(8,128)(2,1)S(1)}, bf16[4,1024,128]{2,1,0:T(8,128)(2,1)}, u32[]{:S(2)}, u32[]{:S(2)}) collective-permute-start(bf16[4,1024,128]{2,1,0:T(8,128)(2,1)S(1)} %collective-permute-done.5), channel_id=1, source_target_pairs={{0,1},{1,2},{2,3},{3,4},{4,5},{5,6},{6,7},{7,8},{8,9},{9,10},{10,1... | collective-permute-start | bytes 3145736 | tf_op jit(solution)/shard_map/ppermute | solution.py:20
  112.2 2.5 %collective-permute-done.12 = bf16[4,1024,128]{2,1,0:T(8,128)(2,1)} collective-permute-done((bf16[4,1024,128]{2,1,0:T(8,128)(2,1)S(1)}, bf16[4,1024,128]{2,1,0:T(8,128)(2,1)}, u32[]{:S(2)}, u32[]{:S(2)}) %collective-permute-start.12) | collective-permute-done | bytes 1048608 | tf_op jit(solution)/shard_map/ppermute | solution.py:22
  114.7 5.3 %collective-permute-start.13 = (bf16[4,1024,128]{2,1,0:T(8,128)(2,1)}, bf16[4,1024,128]{2,1,0:T(8,128)(2,1)}, u32[]{:S(2)}, u32[]{:S(2)}) collective-permute-start(bf16[4,1024,128]{2,1,0:T(8,128)(2,1)} %collective-permute-done.12), channel_id=1, source_target_pairs={{1,0},{2,1},{3,2},{4,3},{5,4},{6,5},{7,6},{8,7},{9,8},{10,9},{11,1... | collective-permute-start | bytes 3145736 | tf_op jit(solution)/shard_map/ppermute | solution.py:22
  120.0 4.0 %collective-permute-done.6 = bf16[4,1024,128]{2,1,0:T(8,128)(2,1)} collective-permute-done((bf16[4,1024,128]{2,1,0:T(8,128)(2,1)S(1)}, bf16[4,1024,128]{2,1,0:T(8,128)(2,1)}, u32[]{:S(2)}, u32[]{:S(2)}) %collective-permute-start.6) | collective-permute-done | bytes 1048608 | tf_op jit(solution)/shard_map/ppermute | solution.py:20
  124.0 2.6 %collective-permute-start.7 = (bf16[4,1024,128]{2,1,0:T(8,128)(2,1)}, bf16[4,1024,128]{2,1,0:T(8,128)(2,1)}, u32[]{:S(2)}, u32[]{:S(2)}) collective-permute-start(bf16[4,1024,128]{2,1,0:T(8,128)(2,1)} %collective-permute-done.6), channel_id=1, source_target_pairs={{0,1},{1,2},{2,3},{3,4},{4,5},{5,6},{6,7},{7,8},{8,9},{9,10},{10,1... | collective-permute-start | bytes 3145736 | tf_op jit(solution)/shard_map/ppermute | solution.py:20
  127.2 23.1 %all_to_all.16 = bf16[16,128,4]{1,2,0:T(4,128)(2,1)S(1)} all-to-all(bf16[16,128,4]{1,2,0:T(4,128)(2,1)S(1)} %broadcast_in_dim.13), channel_id=1, replica_groups=mesh['bank'=16,'zero'=16] {'zero'}, dimensions={0} | all-to-all | bytes 32768 | tf_op jit(solution)/shard_map/all_to_all | solution.py:31
  151.1 6.8 %all-to-all-start.2 = ((bf16[16,2048,4]{1,2,0:T(4,128)(2,1)}), bf16[16,2048,4]{1,2,0:T(4,128)(2,1)S(1)}, u32[]{:S(2)}, u32[]{:S(2)}) async-start(bf16[16,2048,4]{1,2,0:T(4,128)(2,1)} %broadcast_in_dim.14), calls=%async_computation.2 | async-start | bytes 524288 | tf_op jit(solution)/shard_map/all_to_all | solution.py:31
  157.9 8.1 %all-to-all-done.2 = bf16[16,2048,4]{1,2,0:T(4,128)(2,1)S(1)} async-done(((bf16[16,2048,4]{1,2,0:T(4,128)(2,1)}), bf16[16,2048,4]{1,2,0:T(4,128)(2,1)S(1)}, u32[]{:S(2)}, u32[]{:S(2)}) %all-to-all-start.2) | async-done | bytes 262176 | tf_op jit(solution)/shard_map/all_to_all | solution.py:31
  166.8 1.5 collective-permute-start.14
  168.3 2.3 %bitcast_dynamic-update-slice_fusion.15 = bf16[16,4,1024,128]{3,2,1,0:T(8,128)(2,1)} fusion(bf16[4,1024,128]{2,1,0:T(8,128)(2,1)} %collective-permute-done.7), kind=kLoop, calls=%fused_computation.20 | loop fusion | bytes 2097152
  170.6 2.3 %bitcast_dynamic-update-slice_fusion.14 = bf16[16,4,1024,128]{3,2,1,0:T(8,128)(2,1)} fusion(bf16[16,4,1024,128]{3,2,1,0:T(8,128)(2,1)} %bitcast_dynamic-update-slice_fusion.15, bf16[4,1024,128]{2,1,0:T(8,128)(2,1)} %collective-permute-done.6), kind=kLoop, calls=%fused_computation.19 | loop fusion | bytes 2097152
  172.8 2.3 %bitcast_dynamic-update-slice_fusion.13 = bf16[16,4,1024,128]{3,2,1,0:T(8,128)(2,1)} fusion(bf16[16,4,1024,128]{3,2,1,0:T(8,128)(2,1)} %bitcast_dynamic-update-slice_fusion.14, bf16[4,1024,128]{2,1,0:T(8,128)(2,1)} %copy-done.10), kind=kLoop, calls=%fused_computation.18 | loop fusion | bytes 2097152
  175.1 2.3 %bitcast_dynamic-update-slice_fusion.12 = bf16[16,4,1024,128]{3,2,1,0:T(8,128)(2,1)} fusion(bf16[16,4,1024,128]{3,2,1,0:T(8,128)(2,1)} %bitcast_dynamic-update-slice_fusion.13, bf16[4,1024,128]{2,1,0:T(8,128)(2,1)} %copy-done.9), kind=kLoop, calls=%fused_computation.17 | loop fusion | bytes 2097152
  177.4 2.3 %bitcast_dynamic-update-slice_fusion.11 = bf16[16,4,1024,128]{3,2,1,0:T(8,128)(2,1)} fusion(bf16[16,4,1024,128]{3,2,1,0:T(8,128)(2,1)} %bitcast_dynamic-update-slice_fusion.12, bf16[4,1024,128]{2,1,0:T(8,128)(2,1)} %copy-done.8), kind=kLoop, calls=%fused_computation.16 | loop fusion | bytes 2097152
  179.6 2.3 %bitcast_dynamic-update-slice_fusion.10 = bf16[16,4,1024,128]{3,2,1,0:T(8,128)(2,1)} fusion(bf16[16,4,1024,128]{3,2,1,0:T(8,128)(2,1)} %bitcast_dynamic-update-slice_fusion.11, bf16[4,1024,128]{2,1,0:T(8,128)(2,1)} %copy-done.3), kind=kLoop, calls=%fused_computation.15 | loop fusion | bytes 2097152
  181.9 2.3 %bitcast_dynamic-update-slice_fusion.9 = bf16[16,4,1024,128]{3,2,1,0:T(8,128)(2,1)} fusion(bf16[16,4,1024,128]{3,2,1,0:T(8,128)(2,1)} %bitcast_dynamic-update-slice_fusion.10, bf16[4,1024,128]{2,1,0:T(8,128)(2,1)} %copy-done), kind=kLoop, calls=%fused_computation.14 | loop fusion | bytes 2097152
  184.1 1.0 bitcast_dynamic-update-slice_fusion.8
  185.2 1.0 bitcast_dynamic-update-slice_fusion.7
  186.2 1.0 bitcast_dynamic-update-slice_fusion.6
  187.3 1.0 bitcast_dynamic-update-slice_fusion.5
  188.3 1.0 bitcast_dynamic-update-slice_fusion.4
  189.3 1.0 bitcast_dynamic-update-slice_fusion.3
  190.4 2.3 %bitcast_dynamic-update-slice_fusion.2 = bf16[16,4,1024,128]{3,2,1,0:T(8,128)(2,1)} fusion(bf16[16,4,1024,128]{3,2,1,0:T(8,128)(2,1)} %bitcast_dynamic-update-slice_fusion.3, bf16[4,1024,128]{2,1,0:T(8,128)(2,1)} %collective-permute-done.12), kind=kLoop, calls=%fused_computation.7 | loop fusion | bytes 2097152
  192.6 2.3 %bitcast_dynamic-update-slice_fusion.1 = bf16[16,4,1024,128]{3,2,1,0:T(8,128)(2,1)} fusion(bf16[16,4,1024,128]{3,2,1,0:T(8,128)(2,1)} %bitcast_dynamic-update-slice_fusion.2, bf16[4,1024,128]{2,1,0:T(8,128)(2,1)} %collective-permute-done.13), kind=kLoop, calls=%fused_computation.6 | loop fusion | bytes 2097152
  194.9 1.0 bitcast_dynamic-update-slice_fusion
  196.0 13.0 %gather_fusion = bf16[16,4,1024,128]{3,2,1,0:T(8,128)(2,1)} fusion(bf16[16,4,1024,128]{3,2,1,0:T(8,128)(2,1)} %bitcast_dynamic-update-slice_fusion, s32[1024]{0:T(1024)S(1)} %pad_clamp_fusion), kind=kCustom, calls=%fused_computation | custom fusion | bytes 33554496 | tf_op jit(solution)/shard_map/gather | solution.py:25
  209.0 14.4 %copy_bitcast_fusion = bf16[4,1024,2048]{2,1,0:T(8,128)(2,1)} fusion(bf16[16,4,1024,128]{3,2,1,0:T(8,128)(2,1)} %gather_fusion), kind=kLoop, calls=%fused_computation.1 | loop fusion | bytes 33554432 | tf_op jit(solution)/shard_map/reshape | solution.py:10
  (39 shorter events, 4.2 us)
Async XLA Ops:
  24.6 168.1 %copy-start.11 = (f32[4,1024]{1,0:T(4,128)}, f32[4,1024]{1,0:T(4,128)S(1)}, u32[]{:S(2)}) copy-start(f32[4,1024]{1,0:T(4,128)S(1)} %sqrt.7) | copy-start | bytes 49156
  26.8 11.8 %collective-permute-start = (bf16[4,1024,128]{2,1,0:T(8,128)(2,1)S(1)}, bf16[4,1024,128]{2,1,0:T(8,128)(2,1)S(1)}, u32[]{:S(2)}, u32[]{:S(2)}) collective-permute-start(bf16[4,1024,128]{2,1,0:T(8,128)(2,1)S(1)} %divide_convert_fusion), channel_id=1, source_target_pairs={{0,1},{1,2},{2,3},{3,4},{4,5},{5,6},{6,7},{7,8},{8,9},{9,10},{10,1... | collective-permute-start | bytes 3145736 | tf_op jit(solution)/shard_map/ppermute | solution.py:20
  38.6 14.2 %collective-permute-start.1 = (bf16[4,1024,128]{2,1,0:T(8,128)(2,1)S(1)}, bf16[4,1024,128]{2,1,0:T(8,128)(2,1)S(1)}, u32[]{:S(2)}, u32[]{:S(2)}) collective-permute-start(bf16[4,1024,128]{2,1,0:T(8,128)(2,1)S(1)} %collective-permute-done), channel_id=1, source_target_pairs={{0,1},{1,2},{2,3},{3,4},{4,5},{5,6},{6,7},{7,8},{8,9},{9,10},{10,1... | collective-permute-start | bytes 3145736 | tf_op jit(solution)/shard_map/ppermute | solution.py:20
  41.1 14.5 %collective-permute-start.8 = (bf16[4,1024,128]{2,1,0:T(8,128)(2,1)S(1)}, bf16[4,1024,128]{2,1,0:T(8,128)(2,1)S(1)}, u32[]{:S(2)}, u32[]{:S(2)}) collective-permute-start(bf16[4,1024,128]{2,1,0:T(8,128)(2,1)S(1)} %divide_convert_fusion), channel_id=1, source_target_pairs={{1,0},{2,1},{3,2},{4,3},{5,4},{6,5},{7,6},{8,7},{9,8},{10,9},{11,1... | collective-permute-start | bytes 3145736 | tf_op jit(solution)/shard_map/ppermute | solution.py:22
  52.8 17.3 %copy-start = (bf16[4,1024,128]{2,1,0:T(8,128)(2,1)}, bf16[4,1024,128]{2,1,0:T(8,128)(2,1)S(1)}, u32[]{:S(2)}) copy-start(bf16[4,1024,128]{2,1,0:T(8,128)(2,1)S(1)} %collective-permute-done.1) | copy-start | bytes 3145732
  52.8 14.2 %collective-permute-start.2 = (bf16[4,1024,128]{2,1,0:T(8,128)(2,1)S(1)}, bf16[4,1024,128]{2,1,0:T(8,128)(2,1)S(1)}, u32[]{:S(2)}, u32[]{:S(2)}) collective-permute-start(bf16[4,1024,128]{2,1,0:T(8,128)(2,1)S(1)} %collective-permute-done.1), channel_id=1, source_target_pairs={{0,1},{1,2},{2,3},{3,4},{4,5},{5,6},{6,7},{7,8},{8,9},{9,10},{10,1... | collective-permute-start | bytes 3145736 | tf_op jit(solution)/shard_map/ppermute | solution.py:20
  55.6 14.5 %collective-permute-start.9 = (bf16[4,1024,128]{2,1,0:T(8,128)(2,1)S(1)}, bf16[4,1024,128]{2,1,0:T(8,128)(2,1)S(1)}, u32[]{:S(2)}, u32[]{:S(2)}) collective-permute-start(bf16[4,1024,128]{2,1,0:T(8,128)(2,1)S(1)} %collective-permute-done.8), channel_id=1, source_target_pairs={{1,0},{2,1},{3,2},{4,3},{5,4},{6,5},{7,6},{8,7},{9,8},{10,9},{11,1... | collective-permute-start | bytes 3145736 | tf_op jit(solution)/shard_map/ppermute | solution.py:22
  67.0 17.6 %copy-start.3 = (bf16[4,1024,128]{2,1,0:T(8,128)(2,1)}, bf16[4,1024,128]{2,1,0:T(8,128)(2,1)S(1)}, u32[]{:S(2)}) copy-start(bf16[4,1024,128]{2,1,0:T(8,128)(2,1)S(1)} %collective-permute-done.2) | copy-start | bytes 3145732
  67.0 14.2 %collective-permute-start.3 = (bf16[4,1024,128]{2,1,0:T(8,128)(2,1)S(1)}, bf16[4,1024,128]{2,1,0:T(8,128)(2,1)S(1)}, u32[]{:S(2)}, u32[]{:S(2)}) collective-permute-start(bf16[4,1024,128]{2,1,0:T(8,128)(2,1)S(1)} %collective-permute-done.2), channel_id=1, source_target_pairs={{0,1},{1,2},{2,3},{3,4},{4,5},{5,6},{6,7},{7,8},{8,9},{9,10},{10,1... | collective-permute-start | bytes 3145736 | tf_op jit(solution)/shard_map/ppermute | solution.py:20
  70.1 2.7 %copy-start.1 = (bf16[4,1024,128]{2,1,0:T(8,128)(2,1)}, bf16[4,1024,128]{2,1,0:T(8,128)(2,1)S(1)}, u32[]{:S(2)}) copy-start(bf16[4,1024,128]{2,1,0:T(8,128)(2,1)S(1)} %collective-permute-done.9) | copy-start | bytes 3145732
  70.1 14.5 %collective-permute-start.10 = (bf16[4,1024,128]{2,1,0:T(8,128)(2,1)S(1)}, bf16[4,1024,128]{2,1,0:T(8,128)(2,1)S(1)}, u32[]{:S(2)}, u32[]{:S(2)}) collective-permute-start(bf16[4,1024,128]{2,1,0:T(8,128)(2,1)S(1)} %collective-permute-done.9), channel_id=1, source_target_pairs={{1,0},{2,1},{3,2},{4,3},{5,4},{6,5},{7,6},{8,7},{9,8},{10,9},{11,1... | collective-permute-start | bytes 3145736 | tf_op jit(solution)/shard_map/ppermute | solution.py:22
  81.3 33.4 %copy-start.8 = (bf16[4,1024,128]{2,1,0:T(8,128)(2,1)}, bf16[4,1024,128]{2,1,0:T(8,128)(2,1)S(1)}, u32[]{:S(2)}) copy-start(bf16[4,1024,128]{2,1,0:T(8,128)(2,1)S(1)} %collective-permute-done.3) | copy-start | bytes 3145732
  81.3 14.2 %collective-permute-start.4 = (bf16[4,1024,128]{2,1,0:T(8,128)(2,1)S(1)}, bf16[4,1024,128]{2,1,0:T(8,128)(2,1)S(1)}, u32[]{:S(2)}, u32[]{:S(2)}) collective-permute-start(bf16[4,1024,128]{2,1,0:T(8,128)(2,1)S(1)} %collective-permute-done.3), channel_id=1, source_target_pairs={{0,1},{1,2},{2,3},{3,4},{4,5},{5,6},{6,7},{7,8},{8,9},{9,10},{10,1... | collective-permute-start | bytes 3145736 | tf_op jit(solution)/shard_map/ppermute | solution.py:20
  84.6 3.7 %copy-start.4 = (bf16[4,1024,128]{2,1,0:T(8,128)(2,1)}, bf16[4,1024,128]{2,1,0:T(8,128)(2,1)S(1)}, u32[]{:S(2)}) copy-start(bf16[4,1024,128]{2,1,0:T(8,128)(2,1)S(1)} %collective-permute-done.10) | copy-start | bytes 3145732
  84.6 14.5 %collective-permute-start.11 = (bf16[4,1024,128]{2,1,0:T(8,128)(2,1)S(1)}, bf16[4,1024,128]{2,1,0:T(8,128)(2,1)S(1)}, u32[]{:S(2)}, u32[]{:S(2)}) collective-permute-start(bf16[4,1024,128]{2,1,0:T(8,128)(2,1)S(1)} %collective-permute-done.10), channel_id=1, source_target_pairs={{1,0},{2,1},{3,2},{4,3},{5,4},{6,5},{7,6},{8,7},{9,8},{10,9},{11,1... | collective-permute-start | bytes 3145736 | tf_op jit(solution)/shard_map/ppermute | solution.py:22
  95.5 24.5 %copy-start.9 = (bf16[4,1024,128]{2,1,0:T(8,128)(2,1)}, bf16[4,1024,128]{2,1,0:T(8,128)(2,1)S(1)}, u32[]{:S(2)}) copy-start(bf16[4,1024,128]{2,1,0:T(8,128)(2,1)S(1)} %collective-permute-done.4) | copy-start | bytes 3145732
  95.5 14.2 %collective-permute-start.5 = (bf16[4,1024,128]{2,1,0:T(8,128)(2,1)S(1)}, bf16[4,1024,128]{2,1,0:T(8,128)(2,1)S(1)}, u32[]{:S(2)}, u32[]{:S(2)}) collective-permute-start(bf16[4,1024,128]{2,1,0:T(8,128)(2,1)S(1)} %collective-permute-done.4), channel_id=1, source_target_pairs={{0,1},{1,2},{2,3},{3,4},{4,5},{5,6},{6,7},{7,8},{8,9},{9,10},{10,1... | collective-permute-start | bytes 3145736 | tf_op jit(solution)/shard_map/ppermute | solution.py:20
  99.2 1.0 copy-start.6
  100.1 14.5 %collective-permute-start.12 = (bf16[4,1024,128]{2,1,0:T(8,128)(2,1)S(1)}, bf16[4,1024,128]{2,1,0:T(8,128)(2,1)}, u32[]{:S(2)}, u32[]{:S(2)}) collective-permute-start(bf16[4,1024,128]{2,1,0:T(8,128)(2,1)S(1)} %collective-permute-done.11), channel_id=1, source_target_pairs={{1,0},{2,1},{3,2},{4,3},{5,4},{6,5},{7,6},{8,7},{9,8},{10,9},{11,1... | collective-permute-start | bytes 3145736 | tf_op jit(solution)/shard_map/ppermute | solution.py:22
  109.7 14.2 %copy-start.10 = (bf16[4,1024,128]{2,1,0:T(8,128)(2,1)}, bf16[4,1024,128]{2,1,0:T(8,128)(2,1)S(1)}, u32[]{:S(2)}) copy-start(bf16[4,1024,128]{2,1,0:T(8,128)(2,1)S(1)} %collective-permute-done.5) | copy-start | bytes 3145732
  109.7 14.2 %collective-permute-start.6 = (bf16[4,1024,128]{2,1,0:T(8,128)(2,1)S(1)}, bf16[4,1024,128]{2,1,0:T(8,128)(2,1)}, u32[]{:S(2)}, u32[]{:S(2)}) collective-permute-start(bf16[4,1024,128]{2,1,0:T(8,128)(2,1)S(1)} %collective-permute-done.5), channel_id=1, source_target_pairs={{0,1},{1,2},{2,3},{3,4},{4,5},{5,6},{6,7},{7,8},{8,9},{9,10},{10,1... | collective-permute-start | bytes 3145736 | tf_op jit(solution)/shard_map/ppermute | solution.py:20
  114.7 52.1 %collective-permute-start.13 = (bf16[4,1024,128]{2,1,0:T(8,128)(2,1)}, bf16[4,1024,128]{2,1,0:T(8,128)(2,1)}, u32[]{:S(2)}, u32[]{:S(2)}) collective-permute-start(bf16[4,1024,128]{2,1,0:T(8,128)(2,1)} %collective-permute-done.12), channel_id=1, source_target_pairs={{1,0},{2,1},{3,2},{4,3},{5,4},{6,5},{7,6},{8,7},{9,8},{10,9},{11,1... | collective-permute-start | bytes 3145736 | tf_op jit(solution)/shard_map/ppermute | solution.py:22
  124.0 44.4 %collective-permute-start.7 = (bf16[4,1024,128]{2,1,0:T(8,128)(2,1)}, bf16[4,1024,128]{2,1,0:T(8,128)(2,1)}, u32[]{:S(2)}, u32[]{:S(2)}) collective-permute-start(bf16[4,1024,128]{2,1,0:T(8,128)(2,1)} %collective-permute-done.6), channel_id=1, source_target_pairs={{0,1},{1,2},{2,3},{3,4},{4,5},{5,6},{6,7},{7,8},{8,9},{9,10},{10,1... | collective-permute-start | bytes 3145736 | tf_op jit(solution)/shard_map/ppermute | solution.py:20
  151.1 14.9 %all-to-all-start.2 = ((bf16[16,2048,4]{1,2,0:T(4,128)(2,1)}), bf16[16,2048,4]{1,2,0:T(4,128)(2,1)S(1)}, u32[]{:S(2)}, u32[]{:S(2)}) async-start(bf16[16,2048,4]{1,2,0:T(4,128)(2,1)} %broadcast_in_dim.14), calls=%async_computation.2 | async-start | bytes 524288 | tf_op jit(solution)/shard_map/all_to_all | solution.py:31
  166.8 20.5 %copy-start.2 = (bf16[4,1024,128]{2,1,0:T(8,128)(2,1)S(1)}, bf16[4,1024,128]{2,1,0:T(8,128)(2,1)}, u32[]{:S(2)}) copy-start(bf16[4,1024,128]{2,1,0:T(8,128)(2,1)} %copy-done.1) | copy-start | bytes 3145732
  166.8 21.5 %copy-start.5 = (bf16[4,1024,128]{2,1,0:T(8,128)(2,1)S(1)}, bf16[4,1024,128]{2,1,0:T(8,128)(2,1)}, u32[]{:S(2)}) copy-start(bf16[4,1024,128]{2,1,0:T(8,128)(2,1)} %copy-done.4) | copy-start | bytes 3145732
  166.8 22.6 %copy-start.7 = (bf16[4,1024,128]{2,1,0:T(8,128)(2,1)S(1)}, bf16[4,1024,128]{2,1,0:T(8,128)(2,1)}, u32[]{:S(2)}) copy-start(bf16[4,1024,128]{2,1,0:T(8,128)(2,1)} %copy-done.6) | copy-start | bytes 3145732
  166.8 28.1 %collective-permute-start.14 = (bf16[4,1024,128]{2,1,0:T(8,128)(2,1)}, bf16[4,1024,128]{2,1,0:T(8,128)(2,1)S(1)}, u32[]{:S(2)}, u32[]{:S(2)}) collective-permute-start(bf16[4,1024,128]{2,1,0:T(8,128)(2,1)} %collective-permute-done.13), channel_id=1, source_target_pairs={{1,0},{2,1},{3,2},{4,3},{5,4},{6,5},{7,6},{8,7},{9,8},{10,9},{11,1... | collective-permute-start | bytes 3145736 | tf_op jit(solution)/shard_map/ppermute | solution.py:22
